TPU v7x, 512 devices: a 4x2x32 block of a 4x8x32 slice. The times are simulated.
512 devices in a mesh: grp: 2 (over y), seq: 32 (over z), head: 4 (over x), batch: 2 (over core).
Axes of the slice: x: 4, y: 2, z: 32, core: 2. Of those that a mesh axis runs over, the one named last changes fastest.
The devices are a block of a 4x8x32 slice.
Arguments:
- queries: bfloat16 [64, 64, 128], P(('grp', 'batch'), 'head'), parts along dimension 0, may hold values from -8 to 8
- key_cache: bfloat16 [64, 8, 8192, 128], P(('grp', 'batch'), 'head', 'seq'), parts along dimension 0, may hold values from -5 to 5
- value_cache: bfloat16 [64, 8, 8192, 128], P(('grp', 'batch'), 'head', 'seq'), parts along dimension 0, may hold values from -5 to 5
- gate_logits: float32 [2, 64, 64], P(None, ('grp', 'batch'), 'head'), parts along dimension 1, may hold values from -6 to 6
- lengths: int32 [64], P(('grp', 'batch')), parts along dimension 0, may hold values from 2048 to 8192, as said below
- chosen: int32 [64, 8, 16], P(('grp', 'batch'), 'head'), parts along dimension 0, may hold values from 0 to 63, as said below
- counts: int32 [64, 8], P(('grp', 'batch'), 'head'), parts along dimension 0, may hold values from 1 to 16, as said below
Outputs:
- output: bfloat16 [64, 64, 128], P(('grp', 'batch'), 'head'), parts along dimension 0
There are 2 independent parts, one for each index of `grp`. A program takes and returns all parts, laid end to end along the dimension named above; each array names one. Nothing has to cross between parts.
Inputs may be any that keep to these rules, and one draw needn't show every extreme that they name: `lengths`: every draw has a sequence of the full length 8192. `chosen`: for each sequence and key-value head the first counts entries are distinct blocks that start below the sequence's length, and the first entry is block 0; the entries after them are ignored. `counts`: every draw has a sequence with 16 valid entries for every key-value head.
All inputs are finite; a program needn't handle non-finite values.
Results may differ from a plain program's by a relative error of at most 0.02.
Values may be sent and summed in bfloat16 or wider, within the bound.
A program may use at most 64 MiB of HBM per device.

v0:
```python
import math
import jax
import jax.numpy as jnp
from jax import lax
from jax.sharding import PartitionSpec as P

BLOCK = 128


def collected_together(array, axis):
    leaves = jax.tree.leaves(array)
    sequence = sorted(range(len(leaves)), key=lambda k: -leaves[k].size)
    width = (1, *leaves[sequence[0]].shape)[-1]
    lines = [
        jnp.pad(leaves[k].reshape(-1), (0, -leaves[k].size % width)).reshape(-1, width)
        for k in sequence
    ]
    both, at, found = (lax.all_gather(jnp.concatenate(lines), axis), 0, {})
    for k, line in zip(sequence, lines):
        piece = both[:, at : at + len(line)].reshape(len(both), -1)
        found[k] = piece[:, : leaves[k].size].reshape(-1, *leaves[k].shape)
        at += len(line)
    numbers = iter(range(len(leaves)))
    return jax.tree.map(lambda _: found[next(numbers)], array)


def combined_all(array, axis, join):
    gathered = collected_together(
        jax.tree.map(
            lambda a, kind: a.astype(kind), array, (jnp.bfloat16, jnp.bfloat16, jnp.bfloat16)
        ),
        axis,
    )

    def take(source):
        return jax.tree.map(
            lambda a, own: lax.dynamic_index_in_dim(a, source, 0, False).astype(own.dtype),
            gathered,
            array,
        )

    return lax.fori_loop(
        1, lax.axis_size(axis), lambda source, state: join(state, take(source)), take(0)
    )


def softmax_terms(query_rows, key_rows, value_rows, live_mask, score_scale):
    scores = (
        jnp.einsum("pgd,pnd->pgn", query_rows, key_rows, preferred_element_type=jnp.float32)
        * score_scale
    )
    scores = jnp.where(live_mask[:, None, :], scores, -1e30)
    row_max = jnp.max(scores, axis=2)
    weights = jnp.where(live_mask[:, None, :], jnp.exp(scores - row_max[:, :, None]), 0.0)
    weight_sum = jnp.sum(weights, axis=2)
    summed = jnp.einsum(
        "pgn,pnd->pgd", weights.astype(jnp.bfloat16), value_rows, preferred_element_type=jnp.float32
    )
    return (row_max, weight_sum, summed)


def combine(first, second):
    merged = []
    for index in range(0, len(first), 3):
        row_max = jnp.maximum(first[index], second[index])
        factor_first = jnp.exp(first[index] - row_max)
        factor_second = jnp.exp(second[index] - row_max)
        merged.append(row_max)
        merged.append(first[index + 1] * factor_first + second[index + 1] * factor_second)
        merged.append(
            first[index + 2] * factor_first[:, :, None]
            + second[index + 2] * factor_second[:, :, None]
        )
    return tuple(merged)


def finish(weight_sum, summed):
    return summed / weight_sum[:, :, None]


def pool_blocks(key_rows, value_rows, pair_lengths, first_block):
    pair_count, tokens, head_width = key_rows.shape
    block_count = tokens // BLOCK
    position = first_block * BLOCK + jnp.arange(tokens, dtype=jnp.int32)
    live_mask = position[None, :] < pair_lengths[:, None]
    token_ones = live_mask.astype(jnp.bfloat16).reshape(pair_count, block_count, BLOCK)
    starts = (first_block + jnp.arange(block_count, dtype=jnp.int32)) * BLOCK
    filled = jnp.clip(pair_lengths[:, None] - starts[None, :], 0, BLOCK)
    root_fill = jnp.sqrt(jnp.maximum(filled, 1).astype(jnp.float32))[:, :, None]
    key_sums = jnp.einsum(
        "pjt,pjtd->pjd",
        token_ones,
        key_rows.reshape(pair_count, block_count, BLOCK, head_width),
        preferred_element_type=jnp.float32,
    )
    value_sums = jnp.einsum(
        "pjt,pjtd->pjd",
        token_ones,
        value_rows.reshape(pair_count, block_count, BLOCK, head_width),
        preferred_element_type=jnp.float32,
    )
    pooled_keys = (key_sums / root_fill).astype(jnp.bfloat16)
    pooled_values = (value_sums / root_fill).astype(jnp.bfloat16)
    return (live_mask, filled > 0, pooled_keys, pooled_values)


def picked_tokens(live_mask, chosen_rows, count_rows, first_block):
    pair_count, tokens = live_mask.shape
    block_count = tokens // BLOCK
    block_ids = first_block + jnp.arange(block_count, dtype=jnp.int32)
    slot_live = jnp.arange(chosen_rows.shape[1], dtype=jnp.int32)[None, :] < count_rows[:, None]
    picked = jnp.any(
        (chosen_rows[:, :, None] == block_ids[None, None, :]) & slot_live[:, :, None], axis=1
    )
    spread = jnp.broadcast_to(picked[:, :, None], (pair_count, block_count, BLOCK)).reshape(
        pair_count, tokens
    )
    return live_mask & spread


def blend_gates(compressed, selected, gate_pairs):
    mixed = gate_pairs[0][:, :, None] * compressed + gate_pairs[1][:, :, None] * selected
    return mixed.astype(jnp.bfloat16)


def on_device(queries, key_cache, value_cache, gate_logits, lengths, chosen, counts):
    batch_rows, head_count, context, head_width = key_cache.shape
    pair_count = batch_rows * head_count
    group_size = queries.shape[1] // head_count
    score_scale = 1.0 / math.sqrt(head_width)
    query_rows = queries.reshape(pair_count, group_size, head_width)
    pair_keys = key_cache.reshape(pair_count, context, head_width)
    pair_values = value_cache.reshape(pair_count, context, head_width)
    pair_lengths = jnp.broadcast_to(lengths[:, None], (batch_rows, head_count)).reshape(pair_count)
    pair_chosen = chosen.reshape(pair_count, chosen.shape[2])
    pair_counts = counts.reshape(pair_count)
    gate_pairs = jax.nn.sigmoid(gate_logits.reshape(2, pair_count, group_size))
    local_blocks = context // BLOCK
    first_block = lax.axis_index("seq") * local_blocks
    live_mask, block_live, pooled_keys, pooled_values = pool_blocks(
        pair_keys, pair_values, pair_lengths, first_block
    )
    token_mask = picked_tokens(live_mask, pair_chosen, pair_counts, first_block)
    all_keys, all_values = (
        lax.all_gather(pooled_keys, "seq", axis=1, tiled=True),
        lax.all_gather(pooled_values, "seq", axis=1, tiled=True),
    )
    all_starts = jnp.arange(all_keys.shape[1], dtype=jnp.int32) * BLOCK
    all_live = all_starts[None, :] < pair_lengths[:, None]
    s_max, s_sum, s_val = softmax_terms(query_rows, pair_keys, pair_values, token_mask, score_scale)
    merged = combined_all((s_max, s_sum, s_val), "seq", combine)
    c_max, c_sum, c_val = softmax_terms(query_rows, all_keys, all_values, all_live, score_scale)
    output = blend_gates(finish(c_sum, c_val), finish(merged[1], merged[2]), gate_pairs)
    return output.reshape(batch_rows, head_count * group_size, head_width)


def solution(mesh):
    return jax.shard_map(
        on_device,
        mesh=mesh,
        in_specs=(
            P(("grp", "batch"), "head", None),
            P(("grp", "batch"), "head", "seq", None),
            P(("grp", "batch"), "head", "seq", None),
            P(None, ("grp", "batch"), "head"),
            P(("grp", "batch")),
            P(("grp", "batch"), "head", None),
            P(("grp", "batch"), "head"),
        ),
        out_specs=P(("grp", "batch"), "head", None),
        check_vma=False,
    )
```

profile of v0, /device:TPU:36, one launch (start us, length us, event | category | flops | bytes accessed | tf_op | source)
XLA Modules:
  0.0 226.8 jit_solution(120527223969621659)
XLA Ops:
  6.6 0.9 broadcast_in_dim.71
  7.5 0.8 copy.48
  8.4 0.8 copy.47
  9.6 1.7 fusion.34
  12.1 0.6 maximum_bitcast_fusion
  13.3 2.3 fusion.22
  15.6 0.7 fusion.24
  16.3 98.2 %all_gather.12 = bf16[32,64,128]{2,0,1:T(8,128)(2,1)S(1)} all-gather(bf16[32,2,128]{2,0,1:T(8,128)(2,1)S(1)} %get-tuple-element.236), channel_id=1, replica_groups=mesh['grp'=2,'seq'=32,'head'=4,'batch'=2] {'seq'}, dimensions={1}, use_global_device_ids=true | all-gather | bytes 540672 | tf_op jit(solution)/shard_map/all_gather | solution.py:145
  114.5 0.6 fusion.35
  115.1 54.7 %all_gather.13 = bf16[32,64,128]{2,0,1:T(8,128)(2,1)S(1)} all-gather(bf16[32,2,128]{2,0,1:T(8,128)(2,1)S(1)} %get-tuple-element.237), channel_id=1, replica_groups=mesh['grp'=2,'seq'=32,'head'=4,'batch'=2] {'seq'}, dimensions={1}, use_global_device_ids=true | all-gather | bytes 540672 | tf_op jit(solution)/shard_map/all_gather | solution.py:146
  169.8 5.3 %all-gather.4.cloned.1.call-done = bf16[32,260,128]{2,1,0:T(8,128)(2,1)} async-done(((bf16[1,260,128]{2,1,0:T(8,128)(2,1)}), bf16[32,260,128]{2,1,0:T(8,128)(2,1)}) %all-gather.4.cloned.1.call-update) | async-done | bytes 2129936 | tf_op jit(solution)/shard_map/all_gather | solution.py:18
  175.1 0.9 fusion.32
  176.6 0.8 slice_convert_fusion
  177.7 3.1 %slice_bitcast_fusion = bf16[32,32,8,128]{3,2,1,0:T(8,128)(2,1)} fusion(bf16[32,260,128]{2,1,0:T(8,128)(2,1)} %all-gather.4.cloned.1.call-done), kind=kLoop, calls=%fused_computation.9 | loop fusion | bytes 4194304 | tf_op jit(solution)/shard_map/reshape;reshape | solution.py:21
  180.8 0.8 fusion.26
  181.7 37.2 %while.19 = (s32[]{:T(128)}, f32[32,8]{0,1:T(8,128)S(1)}, f32[32,8]{0,1:T(8,128)S(1)}, f32[32,8,128]{2,1,0:T(8,128)S(1)}, bf16[32,32,8]{1,2,0:T(8,128)(2,1)S(1)}...) while((s32[]{:T(128)}, f32[32,8]{0,1:T(8,128)S(1)}, ...), condition=%wide.region_6.7_spmd, body=%wide.region_5.6_spmd.sunk | while | flops 133125 | bytes 341143 | solution.py:42
  181.9 1.0 fusion.48
  183.1 1.0 fusion.48
  184.3 1.0 fusion.48
  185.5 1.0 fusion.48
  186.7 1.0 fusion.48
  187.9 1.0 fusion.48
  189.1 1.0 fusion.48
  190.3 1.0 fusion.48
  191.5 1.0 fusion.48
  192.7 1.0 fusion.48
  193.9 1.0 fusion.48
  195.1 1.0 fusion.48
  196.3 1.0 fusion.48
  197.5 1.0 fusion.48
  198.7 1.0 fusion.48
  199.9 1.0 fusion.48
  201.1 1.0 fusion.48
  202.3 1.0 fusion.48
  203.5 1.0 fusion.48
  204.7 1.0 fusion.48
  205.9 1.0 fusion.48
  207.1 1.0 fusion.48
  208.3 1.0 fusion.48
  209.5 1.0 fusion.48
  210.7 1.0 fusion.48
  211.9 1.0 fusion.48
  213.1 1.0 fusion.48
  214.3 1.0 fusion.48
  215.5 1.0 fusion.48
  216.7 1.0 fusion.48
  217.9 1.0 fusion.48
  219.0 0.9 fusion.12
  (136 shorter events, 8.2 us)
Async XLA Ops:
  6.5 3.0 %copy-start = (bf16[16,2,256,128]{3,2,1,0:T(8,128)(2,1)S(1)}, bf16[16,2,256,128]{3,2,1,0:T(8,128)(2,1)}, u32[]{:S(2)}) copy-start(bf16[16,2,256,128]{3,2,1,0:T(8,128)(2,1)} %param.10) | copy-start | bytes 6291460
  6.6 168.6 %all-gather.4.cloned.1.call-start = ((), (), s32[]{:S(2)}) async-start(), calls=%async_computation | async-start | bytes 2230272 | tf_op jit(solution)/shard_map/all_gather | solution.py:18
  9.4 2.1 copy-start.1
  11.3 1.6 copy-start.3
  13.3 101.2 %copy-start.2 = (bf16[16,16,128]{2,1,0:T(8,128)(2,1)S(1)}, bf16[16,16,128]{2,1,0:T(8,128)(2,1)}, u32[]{:S(2)}) copy-start(bf16[16,16,128]{2,1,0:T(8,128)(2,1)} %param.9) | copy-start | bytes 196612
Sparse Core Ops, SparseCore 0:
  13.0 162.1 all-gather.3
where the time goes:
time: 229 us; the launch traced here: 227 us
  blocking collectives  153 us (67%)
  other arithmetic  34.5 us (15%)
  between operations  13.6 us (6%)
  local copies, waits for them, and re-layouts  12.8 us (6%)
  matrix products  6.53 us (3%)
  waiting for transfers between devices  5.39 us (2%)
    all_gather x1, blocking collectives, on_device(): lax.all_gather(pooled_keys, 'seq', axis=1, tiled=True)  98.2 us
    all_gather x1, blocking collectives, on_device(): lax.all_gather(pooled_values, 'seq', axis=1, tiled=True)  54.7 us
    add x31, other arithmetic, combine(): first[index + 2] * factor_first[:, :, None]  31 us
    all_gather x1, waiting for transfers between devices, collected_together(): both, at, found = (lax.all_gather(jnp.concatenate(lines), axis), 0, {})  5.34 us
  transfers between devices with their start and end apart: 1, of which 1 were waited for; matrix products, arithmetic and copies ran while one was open for 2% of the time, Pallas kernels for 0%

commit v1 on v0

--- a/solution.py
+++ b/solution.py
@@ -142,7 +142,9 @@
     )
     token_mask = picked_tokens(live_mask, pair_chosen, pair_counts, first_block)
     all_keys, all_values = (
-        lax.all_gather(pooled_keys, "seq", axis=1, tiled=True),
+        jnp.concatenate(
+            lax.all_to_all(jnp.stack([pooled_keys] * lax.axis_size("seq")), "seq", 0, 0), axis=1
+        ),
         lax.all_gather(pooled_values, "seq", axis=1, tiled=True),
     )
     all_starts = jnp.arange(all_keys.shape[1], dtype=jnp.int32) * BLOCK

time: 229 us -> 261 us (1.14)
  the two profiles are of different devices: /device:TPU:36 before, /device:TPU:38 now
where the time goes in v1:
time: 261 us; the launch traced here: 259 us
  blocking collectives  97.9 us (38%)
  starting transfers between devices  45.8 us (18%)
  waiting for transfers between devices  45 us (17%)
  other arithmetic  34.6 us (13%)
  local copies, waits for them, and re-layouts  14.8 us (6%)
  between operations  13.6 us (5%)
  matrix products  6.57 us (3%)
    all_gather x1, blocking collectives, on_device(): lax.all_gather(pooled_values, 'seq', axis=1, tiled=True)  97.9 us
    all_to_all x1, starting transfers between devices, on_device(): lax.all_to_all(jnp.stack([pooled_keys] * lax.axis_size('seq')), 'seq', 0, 0)  45.8 us
    all_gather x1, waiting for transfers between devices, collected_together(): both, at, found = (lax.all_gather(jnp.concatenate(lines), axis), 0, {})  45 us
    add x31, other arithmetic, combine(): first[index + 2] * factor_first[:, :, None]  31 us
  transfers between devices with their start and end apart: 2, of which 1 were waited for; matrix products, arithmetic and copies ran while one was open for 2% of the time, Pallas kernels for 0%

profile of v1, /device:TPU:38, one launch (start us, length us, event | category | flops | bytes accessed | tf_op | source)
XLA Modules:
  0.0 259.4 jit_solution(4051450664538254495)
XLA Ops:
  6.6 0.9 broadcast_in_dim.71
  7.7 2.2 fusion.21
  9.9 0.6 fusion.23
  10.8 1.3 stack.2
  12.0 45.8 %all-to-all-start = ((bf16[32,32,2,128]{3,2,1,0:T(2,128)(2,1)}), bf16[32,32,2,128]{3,2,1,0:T(2,128)(2,1)S(1)}, u32[]{:S(2)}, u32[]{:S(2)}) async-start(bf16[32,32,2,128]{3,2,1,0:T(2,128)(2,1)} %stack.2), calls=%async_computation | async-start | bytes 1048576 | tf_op jit(solution)/shard_map/all_to_all | solution.py:146
  58.6 0.7 fusion.33
  59.3 0.7 copy-done.1
  61.8 97.9 %all_gather.9 = bf16[32,64,128]{2,0,1:T(8,128)(2,1)S(1)} all-gather(bf16[32,2,128]{2,0,1:T(8,128)(2,1)S(1)} %get-tuple-element.237), channel_id=1, replica_groups=mesh['grp'=2,'seq'=32,'head'=4,'batch'=2] {'seq'}, dimensions={1}, use_global_device_ids=true | all-gather | bytes 540672 | tf_op jit(solution)/shard_map/all_gather | solution.py:148
  159.8 1.4 copy.47
  161.1 1.6 fusion.34
  162.7 45.0 %all-gather.4.cloned.1.call-done = bf16[32,260,128]{2,1,0:T(8,128)(2,1)} async-done(((bf16[1,260,128]{2,1,0:T(8,128)(2,1)}), bf16[32,260,128]{2,1,0:T(8,128)(2,1)}) %all-gather.4.cloned.1.call-update) | async-done | bytes 2129936 | tf_op jit(solution)/shard_map/all_gather | solution.py:18
  207.7 0.9 fusion.31
  209.2 0.7 slice_convert_fusion
  210.2 3.2 %slice_bitcast_fusion = bf16[32,32,8,128]{3,2,1,0:T(8,128)(2,1)} fusion(bf16[32,260,128]{2,1,0:T(8,128)(2,1)} %all-gather.4.cloned.1.call-done), kind=kLoop, calls=%fused_computation.9 | loop fusion | bytes 4194304 | tf_op jit(solution)/shard_map/reshape;reshape | solution.py:21
  213.4 0.8 fusion.25
  214.2 37.3 %while.19 = (s32[]{:T(128)}, f32[32,8]{0,1:T(8,128)S(1)}, f32[32,8]{0,1:T(8,128)S(1)}, f32[32,8,128]{2,1,0:T(8,128)S(1)}, bf16[32,32,8]{1,2,0:T(8,128)(2,1)S(1)}...) while((s32[]{:T(128)}, f32[32,8]{0,1:T(8,128)S(1)}, ...), condition=%wide.region_6.7_spmd, body=%wide.region_5.6_spmd.sunk | while | flops 133125 | bytes 341143 | solution.py:42
  214.4 1.0 fusion.46
  215.6 1.0 fusion.46
  216.8 1.0 fusion.46
  218.0 1.0 fusion.46
  219.2 1.0 fusion.46
  220.4 1.0 fusion.46
  221.6 1.0 fusion.46
  222.8 1.0 fusion.46
  224.0 1.0 fusion.46
  225.2 1.0 fusion.46
  226.4 1.0 fusion.46
  227.6 1.0 fusion.46
  228.8 1.0 fusion.46
  230.0 1.0 fusion.46
  231.2 1.0 fusion.46
  232.4 1.0 fusion.46
  233.6 1.0 fusion.46
  234.8 1.0 fusion.46
  236.1 1.0 fusion.46
  237.3 1.0 fusion.46
  238.5 1.0 fusion.46
  239.7 1.0 fusion.46
  240.9 1.0 fusion.46
  242.1 1.0 fusion.46
  243.3 1.0 fusion.46
  244.5 1.0 fusion.46
  245.7 1.0 fusion.46
  246.9 1.0 fusion.46
  248.1 1.0 fusion.46
  249.3 1.0 fusion.46
  250.5 1.0 fusion.46
  251.6 0.9 fusion.12
  (144 shorter events, 9.1 us)
Async XLA Ops:
  6.5 3.3 %copy-start = (bf16[16,2,256,128]{3,2,1,0:T(8,128)(2,1)S(1)}, bf16[16,2,256,128]{3,2,1,0:T(8,128)(2,1)}, u32[]{:S(2)}) copy-start(bf16[16,2,256,128]{3,2,1,0:T(8,128)(2,1)} %param.10) | copy-start | bytes 6291460
  9.9 48.0 %copy-start.5 = (s32[16,2]{0,1:T(2,128)S(1)}, s32[16,2]{0,1:T(2,128)}, u32[]{:S(2)}) copy-start(s32[16,2]{0,1:T(2,128)} %param.15) | copy-start | bytes 388
  9.9 48.2 %copy-start.3 = (s32[16,2,16]{2,1,0:T(2,128)S(1)}, s32[16,2,16]{2,1,0:T(2,128)}, u32[]{:S(2)}) copy-start(s32[16,2,16]{2,1,0:T(2,128)} %param.14) | copy-start | bytes 6148
  9.9 48.7 %copy-start.2 = (bf16[16,16,128]{2,1,0:T(8,128)(2,1)S(1)}, bf16[16,16,128]{2,1,0:T(8,128)(2,1)}, u32[]{:S(2)}) copy-start(bf16[16,16,128]{2,1,0:T(8,128)(2,1)} %param.9) | copy-start | bytes 196612
  12.0 147.7 %all-to-all-start = ((bf16[32,32,2,128]{3,2,1,0:T(2,128)(2,1)}), bf16[32,32,2,128]{3,2,1,0:T(2,128)(2,1)S(1)}, u32[]{:S(2)}, u32[]{:S(2)}) async-start(bf16[32,32,2,128]{3,2,1,0:T(2,128)(2,1)} %stack.2), calls=%async_computation | async-start | bytes 1048576 | tf_op jit(solution)/shard_map/all_to_all | solution.py:146
  57.8 149.9 %all-gather.4.cloned.1.call-start = ((), (), s32[]{:S(2)}) async-start(), calls=%async_computation.1 | async-start | bytes 2230272 | tf_op jit(solution)/shard_map/all_gather | solution.py:18
  58.4 1.6 copy-start.1
  59.3 2.2 copy-start.4
Sparse Core Ops, SparseCore 0:
  61.7 145.9 all-gather.3
